TPU v7x, 32 devices: a whole 2x2x4 slice. The times are simulated.
32 devices in a mesh: groups: 2 (over x), freq: 16 (over z, y, core).
Axes of the slice: x: 2, y: 2, z: 4, core: 2. Of those that a mesh axis runs over, the one named last changes fastest.
Arguments:
- traces: bfloat16 [1024, 2048, 32], P('freq', None, 'groups'), parts along dimension 2, may hold values from -6 to 6
- freq_index: int32 [16], replicated, may hold values from 1 to 511
- block_map: int32 [64, 64], replicated, may hold values 0 or 1
- green_rec: bfloat16 [16, 2, 2048, 1536], P('freq', None, None, 'groups'), parts along dimension 3, may hold values from -0.1875 to 0.1875
- green_src: bfloat16 [16, 2, 16, 1536], P('freq', None, None, 'groups'), parts along dimension 3, may hold values from -0.25 to 0.25
Outputs:
- image: float32 [1536], P(('groups', 'freq')), parts along dimension 0
There are 2 independent parts, one for each index of `groups`. A program takes and returns all parts, laid end to end along the dimension named above; an argument that names none is the same for every part. Nothing has to cross between parts.
Inputs may be any that keep to these rules, and one draw needn't show every extreme that they name: `freq_index`: frequency bins; they may repeat. `block_map`: 1 where a receiver block lies in an image tile's aperture.
All inputs are finite; a program needn't handle non-finite values.
Results may differ from a plain program's by a relative error of at most 0.0038.
Values may be sent and summed in bfloat16 or wider, within the bound.
A program may use at most 64 MiB of HBM per device.

v0:
```python
import math

import jax
import jax.numpy as jnp
from jax import lax
from jax.sharding import PartitionSpec as P


def dft_table(freq_index, length):
    sample_index = jnp.arange(length, dtype=jnp.int32)
    phases = freq_index[:, None] * sample_index[None, :] % length
    angles = phases.astype(jnp.float32) * jnp.float32(2.0 * math.pi / length)
    stacked = jnp.stack((jnp.cos(angles), -jnp.sin(angles)), axis=1)
    return stacked.reshape(freq_index.shape[0] * 2, length).astype(jnp.bfloat16)


def expand_map(block_map, receivers, points):
    row_span = receivers // block_map.shape[0]
    col_span = points // block_map.shape[1]
    return jnp.repeat(jnp.repeat(block_map, row_span, axis=0), col_span, axis=1).astype(
        jnp.bfloat16
    )


def transform(cos_table, records, length):
    spectrum = jnp.dot(cos_table, records.reshape(length, -1), preferred_element_type=jnp.float32)
    return (spectrum * (1.0 / math.sqrt(length))).astype(jnp.bfloat16)


def back_project(spectra, masked):
    swapped = jnp.stack((spectra[:, 1], -spectra[:, 0]), axis=1)
    blocks = jnp.stack((spectra, swapped), axis=1)
    return jnp.einsum("fcrx,focrs->fosx", masked, blocks, preferred_element_type=jnp.float32)


def body(traces, freq_index, block_map, green_rec, green_src):
    shards = lax.axis_size("freq")
    length = traces.shape[0] * shards
    receivers = traces.shape[1]
    shots = traces.shape[2]
    freqs = freq_index.shape[0]
    cos_table = dft_table(freq_index, length)
    masked = green_rec * expand_map(block_map, receivers, green_rec.shape[3])[None, None]
    regrouped = lax.all_to_all(traces, "freq", split_axis=2, concat_axis=0, tiled=True)
    spectrum = transform(cos_table, regrouped, length).reshape(freqs, 2, receivers, shots // shards)
    gathered = lax.all_to_all(spectrum, "freq", split_axis=0, concat_axis=3, tiled=True)
    back_field = back_project(gathered, masked)
    partial_image = jnp.sum(green_src.astype(jnp.float32) * back_field, axis=(0, 1, 2))
    return lax.psum_scatter(partial_image, "freq", scatter_dimension=0, tiled=True)


def solution(mesh):
    in_specs = (
        P("freq", None, "groups"),
        P(),
        P(),
        P("freq", None, None, "groups"),
        P("freq", None, None, "groups"),
    )
    out_specs = P(("groups", "freq"))
    return jax.shard_map(body, mesh=mesh, in_specs=in_specs, out_specs=out_specs, check_vma=False)
```

profile of v0, /device:TPU:0, one launch (start us, length us, event | category | flops | bytes accessed | tf_op | source)
XLA Modules:
  0.0 166.9 jit_solution(11297971137079490773)
XLA Ops:
  0.0 6.4 %copy.26 = bf16[64,2048,16]{1,0,2:T(8,128)(2,1)} copy(bf16[64,2048,16]{1,2,0:T(8,128)(2,1)} %param.5) | data formatting | bytes 8388608 | tf_op args[0]
  6.4 0.0 copy-start.2
  6.5 7.6 %all-to-all-start = ((bf16[64,2048,16]{1,0,2:T(8,128)(2,1)}), bf16[64,2048,16]{1,0,2:T(8,128)(2,1)}, u32[]{:S(2)}, u32[]{:S(2)}) async-start(bf16[64,2048,16]{1,0,2:T(8,128)(2,1)} %copy.26), calls=%async_computation | async-start | bytes 8388608 | tf_op jit(solution)/shard_map/all_to_all | solution.py:44
  14.1 0.0 copy-done.2
  14.1 0.0 copy-start.1
  14.1 0.3 cosine_convert_fusion
  14.4 0.1 copy.25
  14.6 77.0 %all-to-all-done = bf16[64,2048,16]{1,0,2:T(8,128)(2,1)} async-done(((bf16[64,2048,16]{1,0,2:T(8,128)(2,1)}), bf16[64,2048,16]{1,0,2:T(8,128)(2,1)}, u32[]{:S(2)}, u32[]{:S(2)}) %all-to-all-start) | async-done | bytes 4194336 | tf_op jit(solution)/shard_map/all_to_all | solution.py:44
  91.6 3.0 %fusion.4 = bf16[32,2048]{1,0:T(8,128)(2,1)S(1)} fusion(bf16[32,1024]{1,0:T(8,128)(2,1)S(1)} %convert_element_type.47, bf16[1024,2048]{1,0:T(8,128)(2,1)} %bitcast.2), kind=kOutput, calls=%fused_computation.5 | convolution fusion | flops 134348800 | bytes 4390912 | tf_op jit(solution)/shard_map/dot_general | solution.py:26
  94.6 0.8 reshape.132
  95.4 19.6 %all-to-all-start.1 = ((bf16[16,2,2048,1]{2,1,3,0:T(2,128)(2,1)}), bf16[16,2,2048,1]{2,1,3,0:T(2,128)(2,1)S(1)}, u32[]{:S(2)}, u32[]{:S(2)}) async-start(bf16[16,2,2048,1]{2,1,3,0:T(2,128)(2,1)} %bitcast.3), calls=%async_computation.1 | async-start | bytes 262144 | tf_op jit(solution)/shard_map/all_to_all | solution.py:46
  115.0 0.0 copy-done.1
  115.1 0.1 broadcast_in_dim.4
  115.1 0.2 copy.29
  115.3 2.5 %broadcast_in_dim.10 = bf16[2048,64,12]{0,2,1:T(8,128)(2,1)} broadcast(bf16[2048,64]{0,1:T(8,128)(2,1)S(1)} %copy.29), dimensions={0,1} | broadcast | bytes 3407872 | tf_op jit(solution)/shard_map/broadcast_in_dim | solution.py:20
  117.8 6.2 %convert_element_type.51 = bf16[2048,768]{0,1:T(8,128)(2,1)} reshape(bf16[2048,64,12]{0,2,1:T(8,128)(2,1)} %broadcast_in_dim.10) | data formatting | bytes 6291456 | tf_op jit(solution)/shard_map/convert_element_type | solution.py:20
  124.0 0.0 copy-start.3
  124.0 0.0 copy-start
  124.0 3.2 %copy.30 = bf16[2048,768]{1,0:T(8,128)(2,1)S(1)} copy(bf16[2048,768]{0,1:T(8,128)(2,1)} %convert_element_type.51) | data formatting | bytes 6291456 | tf_op jit(solution)/shard_map/convert_element_type | solution.py:20
  127.2 0.0 copy-done.3
  127.2 0.6 dynamic-slice
  128.4 0.0 all-to-all-done.1
  128.5 0.0 copy-done
  128.5 4.0 %fusion.11 = f32[768]{0:T(1024)S(1)} fusion(bf16[1,2,2048,768]{3,2,1,0:T(8,128)(2,1)} %param.8, bf16[2048,768]{1,0:T(8,128)(2,1)S(1)} %copy.30, bf16[1,1,2,2048,16]{3,4,2,1,0:T(8,128)(2,1)S(1)} %maximum_bitcast_fusion.2, bf16[1,1,2,2048,16]{3,4,2,1,0:T(8,128)(2,1)S(1)} %bitcast.47, bf16[1,2,16,768]{3,2,1,0:T(8,128)(2,1)S(1)} %copy-done), kind=kOutput, calls=%fused_computation.8 | convolution fusion | flops 204676352 | bytes 9751552 | tf_op jit(solution)/shard_map/fcrx,focrs->fosx/dot_general | solution.py:33
  132.5 33.8 %all-reduce = f32[768]{0:T(1024)S(1)} all-reduce(f32[768]{0:T(1024)S(1)} %fusion.11), channel_id=2, replica_groups=mesh['groups'=2,'freq'=16] {'freq'}, use_global_device_ids=true, to_apply=%region_1.2.clone | all-reduce | flops 768 | bytes 6144
  166.3 0.6 dynamic-slice.1
  (6 shorter events, 0.1 us)
Async XLA Ops:
  6.4 7.6 %copy-start.2 = (s32[16]{0:T(128)S(1)}, s32[16]{0:T(128)}, u32[]{:S(2)}) copy-start(s32[16]{0:T(128)} %param.6) | copy-start | bytes 196
  6.5 85.1 %all-to-all-start = ((bf16[64,2048,16]{1,0,2:T(8,128)(2,1)}), bf16[64,2048,16]{1,0,2:T(8,128)(2,1)}, u32[]{:S(2)}, u32[]{:S(2)}) async-start(bf16[64,2048,16]{1,0,2:T(8,128)(2,1)} %copy.26), calls=%async_computation | async-start | bytes 8388608 | tf_op jit(solution)/shard_map/all_to_all | solution.py:44
  14.1 101.0 %copy-start.1 = (s32[64,64]{1,0:T(8,128)S(1)}, s32[64,64]{1,0:T(8,128)}, u32[]{:S(2)}) copy-start(s32[64,64]{1,0:T(8,128)} %param.7) | copy-start | bytes 49156
  95.4 33.1 %all-to-all-start.1 = ((bf16[16,2,2048,1]{2,1,3,0:T(2,128)(2,1)}), bf16[16,2,2048,1]{2,1,3,0:T(2,128)(2,1)S(1)}, u32[]{:S(2)}, u32[]{:S(2)}) async-start(bf16[16,2,2048,1]{2,1,3,0:T(2,128)(2,1)} %bitcast.3), calls=%async_computation.1 | async-start | bytes 262144 | tf_op jit(solution)/shard_map/all_to_all | solution.py:46
  124.0 3.2 %copy-start.3 = (u32[32]{0:T(128)S(1)}, u32[32]{0:T(128)}, u32[]{:S(2)}) copy-start(u32[32]{0:T(128)} %constant.25) | copy-start | bytes 388
  124.0 4.6 %copy-start = (bf16[1,2,16,768]{3,2,1,0:T(8,128)(2,1)S(1)}, bf16[1,2,16,768]{3,2,1,0:T(8,128)(2,1)}, u32[]{:S(2)}) copy-start(bf16[1,2,16,768]{3,2,1,0:T(8,128)(2,1)} %param.9) | copy-start | bytes 147460
where the time goes:
time: 168 us; the launch traced here: 167 us
  waiting for transfers between devices  77 us (46%)
  blocking collectives  33.8 us (20%)
  starting transfers between devices  27.2 us (16%)
  local copies, waits for them, and re-layouts  20.6 us (12%)
  matrix products  6.97 us (4%)
    all_to_all x1, waiting for transfers between devices, body(): lax.all_to_all(traces, 'freq', split_axis=2, concat_axis=0, tiled=True)  77 us
    unnamed x1, blocking collectives  33.8 us
    all_to_all x1, starting transfers between devices, body(): lax.all_to_all(spectrum, 'freq', split_axis=0, concat_axis=3, tiled=True)  19.6 us
    convert_element_type x3, local copies, waits for them, and re-layouts, expand_map(): jnp.repeat(jnp.repeat(block_map, row_span, axis=0), col_span, axis=1)  9.56 us
    unnamed x11, local copies, waits for them, and re-layouts  7.64 us
    all_to_all x1, starting transfers between devices, body(): lax.all_to_all(traces, 'freq', split_axis=2, concat_axis=0, tiled=True)  7.6 us
    dot_general x1, matrix products, back_project(): jnp.einsum('fcrx,focrs->fosx', masked, blocks, preferred_element_type=jnp...  3.96 us
  transfers between devices with their start and end apart: 2, of which 1 were waited for; matrix products, arithmetic and copies ran while one was open for 8% of the time, Pallas kernels for 0%

commit v1 on v0

--- a/solution.py
+++ b/solution.py
@@ -1,8 +1,11 @@
+import functools
 import math
 
 import jax
 import jax.numpy as jnp
 from jax import lax
+from jax.experimental import pallas as pl
+from jax.experimental.pallas import tpu as pltpu
 from jax.sharding import PartitionSpec as P
 
 
@@ -49,6 +52,347 @@
     return lax.psum_scatter(partial_image, "freq", scatter_dimension=0, tiled=True)
 
 
+CORES = 2
+ROWS = 2
+CHUNKS = 4
+LANES = 128
+
+
+def seat(cols, row, core):
+    return (cols * ROWS + row) * CORES + core
+
+
+def remote(src, dst, send_sem, recv_sem, target):
+    return pltpu.make_async_remote_copy(
+        src_ref=src,
+        dst_ref=dst,
+        send_sem=send_sem,
+        recv_sem=recv_sem,
+        device_id={"freq": target},
+        device_id_type=pl.DeviceIdType.MESH,
+    )
+
+
+def imaging_kernel(
+    shots,
+    x_ref,
+    fi_ref,
+    map_ref,
+    green_ref,
+    src_ref,
+    out_ref,
+    x_own,
+    x_far,
+    table,
+    y_send,
+    y_own,
+    y_recv,
+    z_send,
+    z_own,
+    z_recv,
+    green_v,
+    src_v,
+    map_v,
+    mask_v,
+    acc,
+    i_send,
+    i_recv,
+    x_sem,
+    load_sem,
+    far_send,
+    far_recv,
+    ys_sem,
+    yr_sem,
+    zs_sem,
+    zr_sem,
+    is_sem,
+    ir_sem,
+):
+    shards = i_send.shape[0]
+    cols = shards // (ROWS * CORES)
+    local_rows, half = x_own.shape
+    samples = local_rows // shots
+    length = samples * shards
+    chunks, band, width = y_own.shape
+    freqs = fi_ref.shape[0]
+    receivers = CORES * half
+    points = acc.shape[1]
+    block = 2 * shots
+    bf16, f32 = jnp.bfloat16, jnp.float32
+
+    me = lax.axis_index("freq")
+    core = lax.rem(me, CORES)
+    row = lax.rem(me // CORES, ROWS)
+    col = me // (CORES * ROWS)
+    mate = seat(col, row, 1 - core)
+    across = seat(col, 1 - row, core)
+
+    barrier = pltpu.get_barrier_semaphore()
+    for step in range(1, shards):
+        pl.semaphore_signal(
+            barrier,
+            inc=1,
+            device_id={"freq": lax.rem(me + step, shards)},
+            device_id_type=pl.DeviceIdType.MESH,
+        )
+
+    def lanes(core_at, k):
+        return pl.ds(pl.multiple_of(core_at * half + k * width, LANES), width)
+
+    def x_load(k):
+        return pltpu.make_async_copy(
+            x_ref.at[:, lanes(core, k)], x_own.at[:, pl.ds(k * width, width)], x_sem.at[k]
+        )
+
+    def far_copy(k):
+        return remote(
+            x_ref.at[:, lanes(1 - core, k)],
+            x_far.at[:, pl.ds(k * width, width)],
+            far_send.at[k],
+            far_recv.at[k],
+            mate,
+        )
+
+    map_load = pltpu.make_async_copy(map_ref, map_v, load_sem.at[0])
+    src_load = pltpu.make_async_copy(src_ref, src_v, load_sem.at[1])
+    green_load = pltpu.make_async_copy(green_ref, green_v, load_sem.at[2])
+    for k in range(chunks):
+        x_load(k).start()
+    map_load.start()
+    src_load.start()
+    green_load.start()
+
+    table_rows = 2 * freqs
+    span = CORES * samples
+    line = lax.broadcasted_iota(jnp.int32, (table_rows, span), 0)
+    column = lax.broadcasted_iota(jnp.int32, (table_rows, span), 1)
+    bins = jnp.zeros((table_rows, span), jnp.int32)
+    for f in range(freqs):
+        place = ((f // CORES) % ROWS * cols + f // (CORES * ROWS)) * CORES + f % CORES
+        bins = jnp.where(line // 2 == place, fi_ref[f], bins)
+    time = jnp.where(column < samples, me * samples + column, (mate - 1) * samples + column)
+    angles = lax.rem(bins * time, length).astype(f32) * f32(2.0 * math.pi / length)
+    small = jnp.where(line % 2 == 0, jnp.cos(angles), -jnp.sin(angles)).astype(bf16)
+    wide = span * shots
+    spread = lax.broadcasted_iota(jnp.int32, (span, wide), 1) // shots == lax.broadcasted_iota(
+        jnp.int32, (span, wide), 0
+    )
+    stretched = jnp.dot(small, jnp.where(spread, 1.0, 0.0).astype(bf16), preferred_element_type=f32)
+    same_shot = lax.broadcasted_iota(jnp.int32, (shots, wide), 1) % shots == lax.broadcasted_iota(
+        jnp.int32, (shots, wide), 0
+    )
+    for r in range(table_rows):
+        spread_row = jnp.broadcast_to(stretched[r : r + 1, :], (shots, wide))
+        table[r * shots : (r + 1) * shots, :] = jnp.where(same_shot, spread_row, 0.0).astype(bf16)
+
+    pl.semaphore_wait(barrier, shards - 1)
+    for k in range(chunks):
+        far_copy(k).start()
+
+    def partial(side, k):
+        rows = pl.ds(pl.multiple_of(side * band, band), band)
+        at = pl.ds(k * width, width)
+        near = jnp.dot(table[rows, :local_rows], x_own[:, at], preferred_element_type=f32)
+        return near + jnp.dot(table[rows, local_rows:], x_far[:, at], preferred_element_type=f32)
+
+    def y_copy(k):
+        return remote(y_send.at[k], y_recv.at[k], ys_sem.at[k], yr_sem.at[k], across)
+
+    for k in range(chunks):
+        x_load(k).wait()
+        far_copy(k).wait_recv()
+        y_send[k] = partial(1 - row, k).astype(bf16)
+        y_copy(k).start()
+    for k in range(chunks):
+        y_own[k] = partial(row, k)
+
+    map_load.wait()
+    tiles = map_v.shape[1]
+    in_tile = lax.broadcasted_iota(jnp.int32, (tiles, points), 1) // (
+        points // tiles
+    ) == lax.broadcasted_iota(jnp.int32, (tiles, points), 0)
+    mask_v[...] = jnp.dot(
+        map_v[...].astype(f32).astype(bf16),
+        jnp.where(in_tile, 1.0, 0.0).astype(bf16),
+        preferred_element_type=f32,
+    )
+    green_load.wait()
+    deep = receivers // map_v.shape[0]
+
+    def mask_block(i, carry):
+        seen = jnp.broadcast_to(mask_v[pl.ds(i, 1), :], (deep, points)).astype(bf16)
+        for part in range(2):
+            at = pl.ds(pl.multiple_of(part * receivers + i * deep, deep), deep)
+            green_v[at, :] = green_v[at, :] * seen
+        return carry
+
+    lax.fori_loop(0, map_v.shape[0], mask_block, 0)
+    acc[...] = jnp.zeros_like(acc)
+
+    def block_rows(col_at, core_at):
+        return pl.ds(pl.multiple_of((col_at * CORES + core_at) * block, block), block)
+
+    peers = [(dc, dk) for dc in range(cols) for dk in range(CORES) if dc or dk]
+
+    def z_copy(k, dc, dk):
+        to_col = lax.rem(col + dc, cols)
+        to_core = lax.rem(core + dk, CORES)
+        return remote(
+            z_send.at[k, block_rows(to_col, to_core), :],
+            z_recv.at[col, :, lanes(core, k)],
+            zs_sem.at[k, dc, dk],
+            zr_sem.at[k, dc, dk],
+            seat(to_col, row, to_core),
+        )
+
+    def z_arrival(k, dc, dk):
+        from_col = lax.rem(col + cols - dc, cols)
+        from_core = lax.rem(core + dk, CORES)
+        here = z_recv.at[from_col, :, lanes(from_core, k)]
+        return remote(here, here, zs_sem.at[k, dc, dk], zr_sem.at[k, dc, dk], mate)
+
+    def scatter(k):
+        y_copy(k).wait_recv()
+        y_own[k] = y_own[k] + y_recv[k].astype(f32)
+        z_send[k] = y_own[k].astype(bf16)
+        for dc, dk in peers:
+            z_copy(k, dc, dk).start()
+        z_own[k] = y_own[k, block_rows(col, core), :]
+
+    def use(spectrum, core_at, k):
+        spectrum = spectrum * f32(1.0 / math.sqrt(length))
+        turned = jnp.concatenate((spectrum[shots:], -spectrum[:shots]), axis=0)
+        first = pl.ds(pl.multiple_of(core_at * half + k * width, width), width)
+        second = pl.ds(pl.multiple_of(receivers + core_at * half + k * width, width), width)
+        acc[...] += jnp.dot(
+            spectrum.astype(bf16), green_v[first, :], preferred_element_type=f32
+        ) + jnp.dot(turned.astype(bf16), green_v[second, :], preferred_element_type=f32)
+
+    def consume(k):
+        for dk in range(CORES):
+            from_core = lax.rem(core + dk, CORES)
+            total = None if dk else z_own[k]
+            for dc in range(cols):
+                if dc or dk:
+                    z_arrival(k, dc, dk).wait_recv()
+                    from_col = lax.rem(col + cols - dc, cols)
+                    term = z_recv[from_col, :, lanes(from_core, k)].astype(f32)
+                    total = term if total is None else total + term
+            use(total, from_core, k)
+
+    for k in range(chunks):
+        scatter(k)
+        if k >= 1:
+            consume(k - 1)
+    consume(chunks - 1)
+
+    src_load.wait()
+    product = src_v[...].astype(f32) * acc[...]
+    folded = product[0:8]
+    for at in range(8, block, 8):
+        folded = folded + product[at : at + 8]
+    flat = jnp.broadcast_to(jnp.sum(folded, axis=0, keepdims=True), (8, points))
+    each = points // shards
+    for d in range(shards):
+        i_send[d] = pltpu.roll(flat, (points - d * each) % points, 1)[0:1, :LANES]
+
+    def i_copy(step):
+        to = lax.rem(me + step, shards)
+        return remote(i_send.at[to], i_recv.at[step], is_sem.at[step], ir_sem.at[step], to)
+
+    for step in range(1, shards):
+        i_copy(step).start()
+    total = i_send[me]
+    for step in range(1, shards):
+        i_copy(step).wait_recv()
+        total = total + i_recv[step]
+    out_ref[...] = total
+
+    for k in range(chunks):
+        far_copy(k).wait_send()
+        y_copy(k).wait_send()
+        for dc, dk in peers:
+            z_copy(k, dc, dk).wait_send()
+    for step in range(1, shards):
+        i_copy(step).wait_send()
+
+
+def fused_body(traces, freq_index, block_map, green_rec, green_src):
+    shards = lax.axis_size("freq")
+    samples, receivers, shots = traces.shape
+    points = green_rec.shape[3]
+    freqs = freq_index.shape[0]
+    cols = shards // (ROWS * CORES)
+    half = receivers // CORES
+    width = half // CHUNKS
+    records = jnp.transpose(traces, (0, 2, 1)).reshape(samples * shots, receivers)
+    green = green_rec.reshape(2 * receivers, points)
+    sources = green_src.reshape(2 * shots, points)
+    band = 2 * freqs * shots // ROWS
+    block = 2 * shots
+    bf16, f32 = jnp.bfloat16, jnp.float32
+    dma = pltpu.SemaphoreType.DMA
+    anywhere = pl.BlockSpec(memory_space=pl.ANY)
+    image = pl.pallas_call(
+        functools.partial(imaging_kernel, shots),
+        out_shape=jax.ShapeDtypeStruct((1, LANES), f32),
+        in_specs=[anywhere, pl.BlockSpec(memory_space=pltpu.SMEM), anywhere, anywhere, anywhere],
+        out_specs=pl.BlockSpec(memory_space=pltpu.VMEM),
+        scratch_shapes=[
+            pltpu.VMEM((samples * shots, half), bf16),
+            pltpu.VMEM((samples * shots, half), bf16),
+            pltpu.VMEM((2 * freqs * shots, CORES * samples * shots), bf16),
+            pltpu.VMEM((CHUNKS, band, width), bf16),
+            pltpu.VMEM((CHUNKS, band, width), f32),
+            pltpu.VMEM((CHUNKS, band, width), bf16),
+            pltpu.VMEM((CHUNKS, band, width), bf16),
+            pltpu.VMEM((CHUNKS, block, width), f32),
+            pltpu.VMEM((cols, block, receivers), bf16),
+            pltpu.VMEM((2 * receivers, points), bf16),
+            pltpu.VMEM((block, points), bf16),
+            pltpu.VMEM(block_map.shape, jnp.int32),
+            pltpu.VMEM((block_map.shape[0], points), f32),
+            pltpu.VMEM((block, points), f32),
+            pltpu.VMEM((shards, 1, LANES), f32),
+            pltpu.VMEM((shards, 1, LANES), f32),
+            dma((CHUNKS,)),
+            dma((3,)),
+            dma((CHUNKS,)),
+            dma((CHUNKS,)),
+            dma((CHUNKS,)),
+            dma((CHUNKS,)),
+            dma((CHUNKS, cols, CORES)),
+            dma((CHUNKS, cols, CORES)),
+            dma((shards,)),
+            dma((shards,)),
+        ],
+        compiler_params=pltpu.CompilerParams(
+            collective_id=0, has_side_effects=True, vmem_limit_bytes=48 * 1024 * 1024
+        ),
+    )(records, freq_index, block_map, green, sources)
+    return image[0, : points // shards]
+
+
+def moves_less(traces, freq_index, green_rec):
+    shards = lax.axis_size("freq")
+    samples, receivers, shots = traces.shape
+    freqs = freq_index.shape[0]
+    return (
+        2 * freqs <= samples
+        and freqs == shards
+        and shards % (ROWS * CORES) == 0
+        and shots % 16 == 0
+        and receivers % (CORES * CHUNKS * LANES) == 0
+        and green_rec.shape[3] % LANES == 0
+        and green_rec.shape[3] // shards <= LANES
+    )
+
+
+def chosen_body(traces, freq_index, block_map, green_rec, green_src):
+    fused = moves_less(traces, freq_index, green_rec)
+    return (fused_body if fused else body)(traces, freq_index, block_map, green_rec, green_src)
+
+
 def solution(mesh):
     in_specs = (
         P("freq", None, "groups"),
@@ -58,4 +402,4 @@
         P("freq", None, None, "groups"),
     )
     out_specs = P(("groups", "freq"))
-    return jax.shard_map(body, mesh=mesh, in_specs=in_specs, out_specs=out_specs, check_vma=False)
+    return jax.shard_map(chosen_body, mesh=mesh, in_specs=in_specs, out_specs=out_specs, check_vma=False)

time: 168 us -> 38 us (0.23)
  waiting for transfers between devices: 77 us -> 0 us
  blocking collectives: 33.8 us -> 0 us
  Pallas kernels: 0 us -> 32.8 us
  starting transfers between devices: 27.2 us -> 0 us
  local copies, waits for them, and re-layouts: 20.6 us -> 4.91 us
  matrix products: 6.97 us -> 0 us
    all_to_all x2 -> x0, waiting for transfers between devices: 77.1 us -> none  [the longest x1 77 us: body(): lax.all_to_all(traces, 'freq', split_axis=2, concat_axis=0, tiled=True)]
    unnamed x1 -> x0, blocking collectives: 33.8 us -> none
    pallas_call x0 -> x1, Pallas kernels: none -> 32.8 us  [fused_body(): pl.pallas_call(functools.partial(imaging_kernel, shots), out_shape=jax.Sh...]
    all_to_all x2 -> x0, starting transfers between devices: 27.2 us -> none  [the longest x1 19.6 us: body(): lax.all_to_all(spectrum, 'freq', split_axis=0, concat_axis=3, tiled=True)]
    convert_element_type x4 -> x0, local copies, waits for them, and re-layouts: 9.59 us -> none  [the longest x3 9.56 us: expand_map(): jnp.repeat(jnp.repeat(block_map, row_span, axis=0), col_span, axis=1)]
    dot_general x2 -> x0, matrix products: 6.97 us -> none  [the longest x1 3.96 us: back_project(): jnp.einsum('fcrx,focrs->fosx', masked, blocks, preferred_element_type=jnp...]
    unnamed x11 -> x8, local copies, waits for them, and re-layouts: 7.64 us -> 4.4 us
    broadcast_in_dim x2 -> x0, local copies, waits for them, and re-layouts: 2.54 us -> none  [the longest x1 2.47 us: expand_map(): jnp.repeat(jnp.repeat(block_map, row_span, axis=0), col_span, axis=1)]
  transfers between devices with their start and end apart: 2 -> 0, of which waited for: 1 -> 0; matrix products, arithmetic and copies ran while one was open for 8% -> 0% of each run, Pallas kernels for 0% -> 0%
where the time goes in v1:
time: 38 us; the launch traced here: 37.7 us
  Pallas kernels  32.8 us (86%)
  local copies, waits for them, and re-layouts  4.91 us (13%)
    pallas_call x1, Pallas kernels, fused_body(): pl.pallas_call(functools.partial(imaging_kernel, shots), out_shape=jax.Sh...  32.8 us
    unnamed x8, local copies, waits for them, and re-layouts  4.4 us

profile of v1, /device:TPU:0, one launch (start us, length us, event | category | flops | bytes accessed | tf_op | source)
XLA Modules:
  0.0 37.7 jit_solution(13749999832733278357)
XLA Ops:
  0.0 0.0 copy-start
  0.0 2.2 %copy-done = bf16[64,2048,16]{1,2,0:T(8,128)(2,1)S(1)} copy-done((bf16[64,2048,16]{1,2,0:T(8,128)(2,1)S(1)}, bf16[64,2048,16]{1,2,0:T(8,128)(2,1)}, u32[]{:S(2)}) %copy-start) | copy-done | bytes 4194328
  2.2 0.0 copy-start.1
  2.2 0.8 %copy-done.1 = bf16[1,2,16,768]{3,2,1,0:T(8,128)(2,1)S(1)} copy-done((bf16[1,2,16,768]{3,2,1,0:T(8,128)(2,1)S(1)}, bf16[1,2,16,768]{3,2,1,0:T(8,128)(2,1)}, u32[]{:S(2)}) %copy-start.1) | copy-done | bytes 49176
  3.0 0.0 copy-start.2
  3.0 0.8 %copy-done.2 = s32[64,64]{1,0:T(8,128)S(1)} copy-done((s32[64,64]{1,0:T(8,128)S(1)}, s32[64,64]{1,0:T(8,128)}, u32[]{:S(2)}) %copy-start.2) | copy-done | bytes 16408
  3.7 0.0 copy-start.3
  3.7 0.7 %copy-done.3 = s32[16]{0:T(128)S(1)} copy-done((s32[16]{0:T(128)S(1)}, s32[16]{0:T(128)}, u32[]{:S(2)}) %copy-start.3) | copy-done | bytes 88
  4.4 32.8 %shard_map.55 = f32[1,128]{1,0:T(1,128)S(1)} custom-call(bf16[1024,2048]{1,0:T(8,128)(2,1)S(1)} %bitcast.7, s32[16]{0:T(128)S(1)} %copy-done.3, s32[64,64]{1,0:T(8,128)S(1)} %copy-done.2, bf16[4096,768]{1,0:T(8,128)(2,1)} %bitcast.9, bf16[32,768]{1,0:T(8,128)(2,1)S(1)} %bitcast.8), custom_call_target="tpu_custom_call" | custom-call | tf_op jit(solution)/shard_map/pallas_call | solution.py:336
  37.2 0.5 %slice_bitcast_fusion = f32[48]{0:T(128)} fusion(f32[1,128]{1,0:T(1,128)S(1)} %shard_map.55), kind=kLoop, calls=%fused_computation | loop fusion | bytes 384 | tf_op jit(solution)/shard_map/squeeze | solution.py:373
Async XLA Ops:
  0.0 2.2 %copy-start = (bf16[64,2048,16]{1,2,0:T(8,128)(2,1)S(1)}, bf16[64,2048,16]{1,2,0:T(8,128)(2,1)}, u32[]{:S(2)}) copy-start(bf16[64,2048,16]{1,2,0:T(8,128)(2,1)} %param.5) | copy-start | bytes 12582916
  2.2 0.8 %copy-start.1 = (bf16[1,2,16,768]{3,2,1,0:T(8,128)(2,1)S(1)}, bf16[1,2,16,768]{3,2,1,0:T(8,128)(2,1)}, u32[]{:S(2)}) copy-start(bf16[1,2,16,768]{3,2,1,0:T(8,128)(2,1)} %param.9) | copy-start | bytes 147460
  3.0 0.8 %copy-start.2 = (s32[64,64]{1,0:T(8,128)S(1)}, s32[64,64]{1,0:T(8,128)}, u32[]{:S(2)}) copy-start(s32[64,64]{1,0:T(8,128)} %map_ref.1) | copy-start | bytes 49156
  3.7 0.7 %copy-start.3 = (s32[16]{0:T(128)S(1)}, s32[16]{0:T(128)}, u32[]{:S(2)}) copy-start(s32[16]{0:T(128)} %fi_ref.1) | copy-start | bytes 196

commit v2 on v1

--- a/solution.py
+++ b/solution.py
@@ -55,6 +55,7 @@
 CORES = 2
 ROWS = 2
 CHUNKS = 4
+LAG = 2
 LANES = 128
 
 
@@ -76,12 +77,13 @@
 def imaging_kernel(
     shots,
     x_ref,
-    fi_ref,
+    fi_hbm,
     map_ref,
     green_ref,
     src_ref,
     out_ref,
-    x_own,
+    fi_ref,
+    x_all,
     x_far,
     table,
     y_send,
@@ -110,7 +112,7 @@
 ):
     shards = i_send.shape[0]
     cols = shards // (ROWS * CORES)
-    local_rows, half = x_own.shape
+    local_rows, half = x_far.shape
     samples = local_rows // shots
     length = samples * shards
     chunks, band, width = y_own.shape
@@ -139,25 +141,26 @@
     def lanes(core_at, k):
         return pl.ds(pl.multiple_of(core_at * half + k * width, LANES), width)
 
-    def x_load(k):
-        return pltpu.make_async_copy(
-            x_ref.at[:, lanes(core, k)], x_own.at[:, pl.ds(k * width, width)], x_sem.at[k]
-        )
+    def x_load(core_at):
+        side = pl.ds(pl.multiple_of(core_at * half, LANES), half)
+        return pltpu.make_async_copy(x_ref.at[:, side], x_all.at[:, side], x_sem.at[core_at])
 
     def far_copy(k):
         return remote(
-            x_ref.at[:, lanes(1 - core, k)],
+            x_all.at[:, lanes(1 - core, k)],
             x_far.at[:, pl.ds(k * width, width)],
-            far_send.at[k],
+            far_send,
             far_recv.at[k],
             mate,
         )
 
+    fi_load = pltpu.make_async_copy(fi_hbm, fi_ref, load_sem.at[3])
     map_load = pltpu.make_async_copy(map_ref, map_v, load_sem.at[0])
     src_load = pltpu.make_async_copy(src_ref, src_v, load_sem.at[1])
     green_load = pltpu.make_async_copy(green_ref, green_v, load_sem.at[2])
-    for k in range(chunks):
-        x_load(k).start()
+    fi_load.start()
+    x_load(1 - core).start()
+    x_load(core).start()
     map_load.start()
     src_load.start()
     green_load.start()
@@ -166,6 +169,7 @@
     span = CORES * samples
     line = lax.broadcasted_iota(jnp.int32, (table_rows, span), 0)
     column = lax.broadcasted_iota(jnp.int32, (table_rows, span), 1)
+    fi_load.wait()
     bins = jnp.zeros((table_rows, span), jnp.int32)
     for f in range(freqs):
         place = ((f // CORES) % ROWS * cols + f // (CORES * ROWS)) * CORES + f % CORES
@@ -186,20 +190,21 @@
         table[r * shots : (r + 1) * shots, :] = jnp.where(same_shot, spread_row, 0.0).astype(bf16)
 
     pl.semaphore_wait(barrier, shards - 1)
+    x_load(1 - core).wait()
     for k in range(chunks):
         far_copy(k).start()
 
     def partial(side, k):
         rows = pl.ds(pl.multiple_of(side * band, band), band)
         at = pl.ds(k * width, width)
-        near = jnp.dot(table[rows, :local_rows], x_own[:, at], preferred_element_type=f32)
+        near = jnp.dot(table[rows, :local_rows], x_all[:, lanes(core, k)], preferred_element_type=f32)
         return near + jnp.dot(table[rows, local_rows:], x_far[:, at], preferred_element_type=f32)
 
     def y_copy(k):
-        return remote(y_send.at[k], y_recv.at[k], ys_sem.at[k], yr_sem.at[k], across)
-
+        return remote(y_send.at[k], y_recv.at[k], ys_sem, yr_sem.at[k], across)
+
+    x_load(core).wait()
     for k in range(chunks):
-        x_load(k).wait()
         far_copy(k).wait_recv()
         y_send[k] = partial(1 - row, k).astype(bf16)
         y_copy(k).start()
@@ -240,16 +245,14 @@
         return remote(
             z_send.at[k, block_rows(to_col, to_core), :],
             z_recv.at[col, :, lanes(core, k)],
-            zs_sem.at[k, dc, dk],
-            zr_sem.at[k, dc, dk],
+            zs_sem,
+            zr_sem.at[k],
             seat(to_col, row, to_core),
         )
 
-    def z_arrival(k, dc, dk):
-        from_col = lax.rem(col + cols - dc, cols)
-        from_core = lax.rem(core + dk, CORES)
-        here = z_recv.at[from_col, :, lanes(from_core, k)]
-        return remote(here, here, zs_sem.at[k, dc, dk], zr_sem.at[k, dc, dk], mate)
+    def z_arrival(k):
+        every = z_send.at[k, pl.ds(0, len(peers) * block), :]
+        return pltpu.make_async_copy(every, every, zr_sem.at[k])
 
     def scatter(k):
         y_copy(k).wait_recv()
@@ -269,12 +272,12 @@
         ) + jnp.dot(turned.astype(bf16), green_v[second, :], preferred_element_type=f32)
 
     def consume(k):
+        z_arrival(k).wait()
         for dk in range(CORES):
             from_core = lax.rem(core + dk, CORES)
             total = None if dk else z_own[k]
             for dc in range(cols):
                 if dc or dk:
-                    z_arrival(k, dc, dk).wait_recv()
                     from_col = lax.rem(col + cols - dc, cols)
                     term = z_recv[from_col, :, lanes(from_core, k)].astype(f32)
                     total = term if total is None else total + term
@@ -282,9 +285,10 @@
 
     for k in range(chunks):
         scatter(k)
-        if k >= 1:
-            consume(k - 1)
-    consume(chunks - 1)
+        if k >= LAG:
+            consume(k - LAG)
+    for k in range(chunks - LAG, chunks):
+        consume(k)
 
     src_load.wait()
     product = src_v[...].astype(f32) * acc[...]
@@ -298,23 +302,20 @@
 
     def i_copy(step):
         to = lax.rem(me + step, shards)
-        return remote(i_send.at[to], i_recv.at[step], is_sem.at[step], ir_sem.at[step], to)
+        return remote(i_send.at[to], i_recv.at[step], is_sem, ir_sem, to)
 
     for step in range(1, shards):
         i_copy(step).start()
     total = i_send[me]
+    others = i_recv.at[pl.ds(1, shards - 1)]
+    pltpu.make_async_copy(others, others, ir_sem).wait()
     for step in range(1, shards):
-        i_copy(step).wait_recv()
         total = total + i_recv[step]
     out_ref[...] = total
 
-    for k in range(chunks):
-        far_copy(k).wait_send()
-        y_copy(k).wait_send()
-        for dc, dk in peers:
-            z_copy(k, dc, dk).wait_send()
-    for step in range(1, shards):
-        i_copy(step).wait_send()
+    z_sent = z_send.at[:, pl.ds(0, len(peers) * block), :]
+    for sent, sem in ((x_far, far_send), (y_send, ys_sem), (z_sent, zs_sem), (others, is_sem)):
+        pltpu.make_async_copy(sent, sent, sem).wait()
 
 
 def fused_body(traces, freq_index, block_map, green_rec, green_src):
@@ -332,14 +333,15 @@
     block = 2 * shots
     bf16, f32 = jnp.bfloat16, jnp.float32
     dma = pltpu.SemaphoreType.DMA
-    anywhere = pl.BlockSpec(memory_space=pl.ANY)
+    outside = pl.BlockSpec(memory_space=pltpu.HBM)
     image = pl.pallas_call(
         functools.partial(imaging_kernel, shots),
         out_shape=jax.ShapeDtypeStruct((1, LANES), f32),
-        in_specs=[anywhere, pl.BlockSpec(memory_space=pltpu.SMEM), anywhere, anywhere, anywhere],
+        in_specs=[outside] * 5,
         out_specs=pl.BlockSpec(memory_space=pltpu.VMEM),
         scratch_shapes=[
-            pltpu.VMEM((samples * shots, half), bf16),
+            pltpu.SMEM(freq_index.shape, jnp.int32),
+            pltpu.VMEM((samples * shots, receivers), bf16),
             pltpu.VMEM((samples * shots, half), bf16),
             pltpu.VMEM((2 * freqs * shots, CORES * samples * shots), bf16),
             pltpu.VMEM((CHUNKS, band, width), bf16),
@@ -355,21 +357,26 @@
             pltpu.VMEM((block, points), f32),
             pltpu.VMEM((shards, 1, LANES), f32),
             pltpu.VMEM((shards, 1, LANES), f32),
+            dma((CORES,)),
+            dma((4,)),
+            dma,
             dma((CHUNKS,)),
-            dma((3,)),
+            dma,
             dma((CHUNKS,)),
+            dma,
             dma((CHUNKS,)),
-            dma((CHUNKS,)),
-            dma((CHUNKS,)),
-            dma((CHUNKS, cols, CORES)),
-            dma((CHUNKS, cols, CORES)),
-            dma((shards,)),
-            dma((shards,)),
+            dma,
+            dma,
         ],
         compiler_params=pltpu.CompilerParams(
             collective_id=0, has_side_effects=True, vmem_limit_bytes=48 * 1024 * 1024
         ),
-    )(records, freq_index, block_map, green, sources)
+    )(
+        *(
+            pltpu.with_memory_space_constraint(array, pltpu.HBM)
+            for array in (records, freq_index, block_map, green, sources)
+        )
+    )
     return image[0, : points // shards]
 
 

time: 38 us -> 31.9 us (0.84)
  local copies, waits for them, and re-layouts: 4.91 us -> 0.51 us
  Pallas kernels: 32.8 us -> 31.2 us
    unnamed x8 -> x0, local copies, waits for them, and re-layouts: 4.4 us -> none
    pallas_call x1, Pallas kernels: 32.8 us -> 31.2 us  [fused_body(): pl.pallas_call(functools.partial(imaging_kernel, shots), out_shape=jax.Sh...]
where the time goes in v2:
time: 31.9 us; the launch traced here: 31.7 us
  Pallas kernels  31.2 us (98%)
  local copies, waits for them, and re-layouts  0.51 us (2%)
    pallas_call x1, Pallas kernels, fused_body(): pl.pallas_call(functools.partial(imaging_kernel, shots), out_shape=jax.Sh...  31.2 us

profile of v2, /device:TPU:0, one launch (start us, length us, event | category | flops | bytes accessed | tf_op | source)
XLA Modules:
  0.0 31.7 jit_solution(160941934443310571)
XLA Ops:
  0.0 31.2 %shard_map.55 = f32[1,128]{1,0:T(1,128)S(1)} custom-call(bf16[1024,2048]{1,0:T(8,128)(2,1)} %bitcast.8, s32[16]{0:T(128)} %fi_hbm.1, s32[64,64]{1,0:T(8,128)} %map_ref.1, bf16[4096,768]{1,0:T(8,128)(2,1)} %bitcast.7, bf16[32,768]{1,0:T(8,128)(2,1)} %bitcast.9), custom_call_target="tpu_custom_call" | custom-call | tf_op jit(solution)/shard_map/pallas_call | solution.py:337
  31.2 0.5 %slice_bitcast_fusion = f32[48]{0:T(128)} fusion(f32[1,128]{1,0:T(1,128)S(1)} %shard_map.55), kind=kLoop, calls=%fused_computation | loop fusion | bytes 384 | tf_op jit(solution)/shard_map/squeeze | solution.py:380

commit v3 on v2

--- a/solution.py
+++ b/solution.py
@@ -54,9 +54,12 @@
 
 CORES = 2
 ROWS = 2
-CHUNKS = 4
-LAG = 2
+LAG = 4
 LANES = 128
+
+
+def bands(half):
+    return tuple((start, LANES) for start in range(0, half, LANES))
 
 
 def seat(cols, row, core):
@@ -115,7 +118,9 @@
     local_rows, half = x_far.shape
     samples = local_rows // shots
     length = samples * shards
-    chunks, band, width = y_own.shape
+    band = y_own.shape[0]
+    steps = bands(half)
+    chunks = len(steps)
     freqs = fi_ref.shape[0]
     receivers = CORES * half
     points = acc.shape[1]
@@ -139,7 +144,7 @@
         )
 
     def lanes(core_at, k):
-        return pl.ds(pl.multiple_of(core_at * half + k * width, LANES), width)
+        return pl.ds(pl.multiple_of(core_at * half + steps[k][0], LANES), steps[k][1])
 
     def x_load(core_at):
         side = pl.ds(pl.multiple_of(core_at * half, LANES), half)
@@ -148,7 +153,7 @@
     def far_copy(k):
         return remote(
             x_all.at[:, lanes(1 - core, k)],
-            x_far.at[:, pl.ds(k * width, width)],
+            x_far.at[:, pl.ds(*steps[k])],
             far_send,
             far_recv.at[k],
             mate,
@@ -196,20 +201,59 @@
 
     def partial(side, k):
         rows = pl.ds(pl.multiple_of(side * band, band), band)
-        at = pl.ds(k * width, width)
+        at = pl.ds(*steps[k])
         near = jnp.dot(table[rows, :local_rows], x_all[:, lanes(core, k)], preferred_element_type=f32)
         return near + jnp.dot(table[rows, local_rows:], x_far[:, at], preferred_element_type=f32)
 
     def y_copy(k):
-        return remote(y_send.at[k], y_recv.at[k], ys_sem, yr_sem.at[k], across)
-
+        at = pl.ds(*steps[k])
+        return remote(y_send.at[:, at], y_recv.at[:, at], ys_sem, yr_sem.at[k], across)
+
+    def send_partial(k):
+        far_copy(k).wait_recv()
+        y_send[:, pl.ds(*steps[k])] = partial(1 - row, k).astype(bf16)
+        y_copy(k).start()
+
+    def keep_partial(k):
+        y_own[:, pl.ds(*steps[k])] = partial(row, k)
+
+    def block_rows(col_at, core_at):
+        return pl.ds(pl.multiple_of((col_at * CORES + core_at) * block, block), block)
+
+    peers = [(dc, dk) for dc in range(cols) for dk in range(CORES) if dc or dk]
+
+    def z_copy(k, dc, dk):
+        to_col = lax.rem(col + dc, cols)
+        to_core = lax.rem(core + dk, CORES)
+        return remote(
+            z_send.at[block_rows(to_col, to_core), pl.ds(*steps[k])],
+            z_recv.at[col, :, lanes(core, k)],
+            zs_sem,
+            zr_sem.at[k],
+            seat(to_col, row, to_core),
+        )
+
+    def scatter(k):
+        y_copy(k).wait_recv()
+        at = pl.ds(*steps[k])
+        y_own[:, at] = y_own[:, at] + y_recv[:, at].astype(f32)
+        z_send[:, at] = y_own[:, at].astype(bf16)
+        for dc, dk in peers:
+            z_copy(k, dc, dk).start()
+        z_own[:, at] = y_own[block_rows(col, core), at]
     x_load(core).wait()
     for k in range(chunks):
-        far_copy(k).wait_recv()
-        y_send[k] = partial(1 - row, k).astype(bf16)
-        y_copy(k).start()
-    for k in range(chunks):
-        y_own[k] = partial(row, k)
+        send_partial(k)
+        if k % 4 == 3:
+            keep_partial(k // 4)
+    early = (chunks + 3) // 4
+    for k in range(chunks // 4, early):
+        keep_partial(k)
+    scatter(0)
+    keep_partial(early)
+    scatter(1)
+    for k in range(early + 1, min(early + 2, chunks)):
+        keep_partial(k)
 
     map_load.wait()
     tiles = map_v.shape[1]
@@ -234,39 +278,15 @@
     lax.fori_loop(0, map_v.shape[0], mask_block, 0)
     acc[...] = jnp.zeros_like(acc)
 
-    def block_rows(col_at, core_at):
-        return pl.ds(pl.multiple_of((col_at * CORES + core_at) * block, block), block)
-
-    peers = [(dc, dk) for dc in range(cols) for dk in range(CORES) if dc or dk]
-
-    def z_copy(k, dc, dk):
-        to_col = lax.rem(col + dc, cols)
-        to_core = lax.rem(core + dk, CORES)
-        return remote(
-            z_send.at[k, block_rows(to_col, to_core), :],
-            z_recv.at[col, :, lanes(core, k)],
-            zs_sem,
-            zr_sem.at[k],
-            seat(to_col, row, to_core),
-        )
-
     def z_arrival(k):
-        every = z_send.at[k, pl.ds(0, len(peers) * block), :]
+        every = z_send.at[pl.ds(0, len(peers) * block), pl.ds(*steps[k])]
         return pltpu.make_async_copy(every, every, zr_sem.at[k])
-
-    def scatter(k):
-        y_copy(k).wait_recv()
-        y_own[k] = y_own[k] + y_recv[k].astype(f32)
-        z_send[k] = y_own[k].astype(bf16)
-        for dc, dk in peers:
-            z_copy(k, dc, dk).start()
-        z_own[k] = y_own[k, block_rows(col, core), :]
 
     def use(spectrum, core_at, k):
         spectrum = spectrum * f32(1.0 / math.sqrt(length))
         turned = jnp.concatenate((spectrum[shots:], -spectrum[:shots]), axis=0)
-        first = pl.ds(pl.multiple_of(core_at * half + k * width, width), width)
-        second = pl.ds(pl.multiple_of(receivers + core_at * half + k * width, width), width)
+        first = lanes(core_at, k)
+        second = lanes(CORES + core_at, k)
         acc[...] += jnp.dot(
             spectrum.astype(bf16), green_v[first, :], preferred_element_type=f32
         ) + jnp.dot(turned.astype(bf16), green_v[second, :], preferred_element_type=f32)
@@ -275,7 +295,7 @@
         z_arrival(k).wait()
         for dk in range(CORES):
             from_core = lax.rem(core + dk, CORES)
-            total = None if dk else z_own[k]
+            total = None if dk else z_own[:, pl.ds(*steps[k])]
             for dc in range(cols):
                 if dc or dk:
                     from_col = lax.rem(col + cols - dc, cols)
@@ -283,8 +303,10 @@
                     total = term if total is None else total + term
             use(total, from_core, k)
 
-    for k in range(chunks):
+    for k in range(2, chunks):
         scatter(k)
+        for at in range(early + 2 * k - 2, min(early + 2 * k, chunks)):
+            keep_partial(at)
         if k >= LAG:
             consume(k - LAG)
     for k in range(chunks - LAG, chunks):
@@ -313,7 +335,7 @@
         total = total + i_recv[step]
     out_ref[...] = total
 
-    z_sent = z_send.at[:, pl.ds(0, len(peers) * block), :]
+    z_sent = z_send.at[pl.ds(0, len(peers) * block), :]
     for sent, sem in ((x_far, far_send), (y_send, ys_sem), (z_sent, zs_sem), (others, is_sem)):
         pltpu.make_async_copy(sent, sent, sem).wait()
 
@@ -325,7 +347,7 @@
     freqs = freq_index.shape[0]
     cols = shards // (ROWS * CORES)
     half = receivers // CORES
-    width = half // CHUNKS
+    chunks = len(bands(half))
     records = jnp.transpose(traces, (0, 2, 1)).reshape(samples * shots, receivers)
     green = green_rec.reshape(2 * receivers, points)
     sources = green_src.reshape(2 * shots, points)
@@ -344,11 +366,11 @@
             pltpu.VMEM((samples * shots, receivers), bf16),
             pltpu.VMEM((samples * shots, half), bf16),
             pltpu.VMEM((2 * freqs * shots, CORES * samples * shots), bf16),
-            pltpu.VMEM((CHUNKS, band, width), bf16),
-            pltpu.VMEM((CHUNKS, band, width), f32),
-            pltpu.VMEM((CHUNKS, band, width), bf16),
-            pltpu.VMEM((CHUNKS, band, width), bf16),
-            pltpu.VMEM((CHUNKS, block, width), f32),
+            pltpu.VMEM((band, half), bf16),
+            pltpu.VMEM((band, half), f32),
+            pltpu.VMEM((band, half), bf16),
+            pltpu.VMEM((band, half), bf16),
+            pltpu.VMEM((block, half), f32),
             pltpu.VMEM((cols, block, receivers), bf16),
             pltpu.VMEM((2 * receivers, points), bf16),
             pltpu.VMEM((block, points), bf16),
@@ -360,11 +382,11 @@
             dma((CORES,)),
             dma((4,)),
             dma,
-            dma((CHUNKS,)),
+            dma((chunks,)),
             dma,
-            dma((CHUNKS,)),
+            dma((chunks,)),
             dma,
-            dma((CHUNKS,)),
+            dma((chunks,)),
             dma,
             dma,
         ],
@@ -389,7 +411,7 @@
         and freqs == shards
         and shards % (ROWS * CORES) == 0
         and shots % 16 == 0
-        and receivers % (CORES * CHUNKS * LANES) == 0
+        and receivers % (CORES * 4 * LANES) == 0
         and green_rec.shape[3] % LANES == 0
         and green_rec.shape[3] // shards <= LANES
     )

time: 31.9 us -> 30.8 us (0.966)
  Pallas kernels: 31.2 us -> 30.2 us
    pallas_call x1, Pallas kernels: 31.2 us -> 30.2 us  [fused_body(): pl.pallas_call(functools.partial(imaging_kernel, shots), out_shape=jax.Sh...]
where the time goes in v3:
time: 30.8 us; the launch traced here: 30.7 us
  Pallas kernels  30.2 us (98%)
  local copies, waits for them, and re-layouts  0.51 us (2%)
    pallas_call x1, Pallas kernels, fused_body(): pl.pallas_call(functools.partial(imaging_kernel, shots), out_shape=jax.Sh...  30.2 us

profile of v3, /device:TPU:0, one launch (start us, length us, event | category | flops | bytes accessed | tf_op | source)
XLA Modules:
  0.0 30.7 jit_solution(8097762802286993849)
XLA Ops:
  0.0 30.2 %shard_map.55 = f32[1,128]{1,0:T(1,128)S(1)} custom-call(bf16[1024,2048]{1,0:T(8,128)(2,1)} %bitcast.8, s32[16]{0:T(128)} %fi_hbm.1, s32[64,64]{1,0:T(8,128)} %map_ref.1, bf16[4096,768]{1,0:T(8,128)(2,1)} %bitcast.7, bf16[32,768]{1,0:T(8,128)(2,1)} %bitcast.9), custom_call_target="tpu_custom_call" | custom-call | tf_op jit(solution)/shard_map/pallas_call | solution.py:359
  30.2 0.5 %slice_bitcast_fusion = f32[48]{0:T(128)} fusion(f32[1,128]{1,0:T(1,128)S(1)} %shard_map.55), kind=kLoop, calls=%fused_computation | loop fusion | bytes 384 | tf_op jit(solution)/shard_map/squeeze | solution.py:402

commit v4 on v3

--- a/solution.py
+++ b/solution.py
@@ -112,6 +112,10 @@
     zr_sem,
     is_sem,
     ir_sem,
+    up_sem,
+    down_sem,
+    pair_sem,
+    row_sem,
 ):
     shards = i_send.shape[0]
     cols = shards // (ROWS * CORES)
@@ -135,13 +139,37 @@
     across = seat(col, 1 - row, core)
 
     barrier = pltpu.get_barrier_semaphore()
-    for step in range(1, shards):
+
+    def tell(sem, target):
         pl.semaphore_signal(
-            barrier,
-            inc=1,
-            device_id={"freq": lax.rem(me + step, shards)},
-            device_id_type=pl.DeviceIdType.MESH,
+            sem, inc=1, device_id={"freq": target}, device_id_type=pl.DeviceIdType.MESH
         )
+
+    tell(barrier, mate)
+    tell(barrier, across)
+
+    @pl.when(col > 0)
+    def _():
+        tell(barrier, seat(col - 1, row, core))
+
+    @pl.when(col < cols - 1)
+    def _():
+        tell(barrier, seat(col + 1, row, core))
+
+    def relay(hop):
+        @pl.when(col == hop)
+        def _():
+            if hop > 0:
+                pl.semaphore_wait(up_sem, 1)
+            if hop < cols - 1:
+                tell(up_sem, seat(col + 1, row, core))
+
+        @pl.when(col == cols - 1 - hop)
+        def _():
+            if hop > 0:
+                pl.semaphore_wait(down_sem, 1)
+            if hop < cols - 1:
+                tell(down_sem, seat(col - 1, row, core))
 
     def lanes(core_at, k):
         return pl.ds(pl.multiple_of(core_at * half + steps[k][0], LANES), steps[k][1])
@@ -194,7 +222,8 @@
         spread_row = jnp.broadcast_to(stretched[r : r + 1, :], (shots, wide))
         table[r * shots : (r + 1) * shots, :] = jnp.where(same_shot, spread_row, 0.0).astype(bf16)
 
-    pl.semaphore_wait(barrier, shards - 1)
+    greeted = 2 + jnp.minimum(col, 1) + jnp.minimum(cols - 1 - col, 1)
+    pl.semaphore_wait(barrier, greeted)
     x_load(1 - core).wait()
     for k in range(chunks):
         far_copy(k).start()
@@ -242,13 +271,21 @@
             z_copy(k, dc, dk).start()
         z_own[:, at] = y_own[block_rows(col, core), at]
     x_load(core).wait()
+    relay(0)
     for k in range(chunks):
         send_partial(k)
+        if k % 2 == 1 and (k + 1) // 2 < cols:
+            relay((k + 1) // 2)
         if k % 4 == 3:
             keep_partial(k // 4)
     early = (chunks + 3) // 4
     for k in range(chunks // 4, early):
         keep_partial(k)
+    for hop in range(chunks // 2 + 1, cols):
+        relay(hop)
+    tell(pair_sem, mate)
+    pl.semaphore_wait(pair_sem, 1)
+    tell(row_sem, across)
     scatter(0)
     keep_partial(early)
     scatter(1)
@@ -326,6 +363,7 @@
         to = lax.rem(me + step, shards)
         return remote(i_send.at[to], i_recv.at[step], is_sem, ir_sem, to)
 
+    pl.semaphore_wait(row_sem, 1)
     for step in range(1, shards):
         i_copy(step).start()
     total = i_send[me]
@@ -389,7 +427,8 @@
             dma((chunks,)),
             dma,
             dma,
-        ],
+        ]
+        + [pltpu.SemaphoreType.REGULAR] * 4,
         compiler_params=pltpu.CompilerParams(
             collective_id=0, has_side_effects=True, vmem_limit_bytes=48 * 1024 * 1024
         ),

time: 30.8 us -> 30.1 us (0.977)
  Pallas kernels: 30.2 us -> 29.4 us
    pallas_call x1, Pallas kernels: 30.2 us -> 29.4 us  [fused_body(): pl.pallas_call(functools.partial(imaging_kernel, shots), out_shape=jax.Sh...]
where the time goes in v4:
time: 30.1 us; the launch traced here: 29.9 us
  Pallas kernels  29.4 us (98%)
  local copies, waits for them, and re-layouts  0.51 us (2%)
    pallas_call x1, Pallas kernels, fused_body(): pl.pallas_call(functools.partial(imaging_kernel, shots), out_shape=jax.Sh...  29.4 us

profile of v4, /device:TPU:0, one launch (start us, length us, event | category | flops | bytes accessed | tf_op | source)
XLA Modules:
  0.0 29.9 jit_solution(6155710515491938523)
XLA Ops:
  0.0 29.4 %shard_map.55 = f32[1,128]{1,0:T(1,128)S(1)} custom-call(bf16[1024,2048]{1,0:T(8,128)(2,1)} %bitcast.8, s32[16]{0:T(128)} %fi_hbm.1, s32[64,64]{1,0:T(8,128)} %map_ref.1, bf16[4096,768]{1,0:T(8,128)(2,1)} %bitcast.7, bf16[32,768]{1,0:T(8,128)(2,1)} %bitcast.9), custom_call_target="tpu_custom_call" | custom-call | tf_op jit(solution)/shard_map/pallas_call | solution.py:397
  29.4 0.5 %slice_bitcast_fusion = f32[48]{0:T(128)} fusion(f32[1,128]{1,0:T(1,128)S(1)} %shard_map.55), kind=kLoop, calls=%fused_computation | loop fusion | bytes 384 | tf_op jit(solution)/shard_map/squeeze | solution.py:441
